TPU v7x, 32 devices: a whole 2x2x4 slice. The times are simulated.
32 devices in a mesh: rows: 4 (over y, x), mp: 8 (over z, core).
Axes of the slice: x: 2, y: 2, z: 4, core: 2. Of those that a mesh axis runs over, the one named last changes fastest.
Arguments:
- tokens: bfloat16 [512, 6144], P('rows', 'mp'), may hold values from -8 to 8
- norm_gain: float32 [6144], replicated, may hold values from 0.25 to 1.75
- hidden_bias: float32 [24576], P('mp'), may hold values from -3 to 3
- weight_in: bfloat16 [6144, 24576], P('rows', 'mp'), may hold values from -0.078125 to 0.078125
- weight_out: bfloat16 [24576, 6144], P('mp', 'rows'), may hold values from -0.0546875 to 0.0546875
Outputs:
- updated: bfloat16 [512, 6144], P('rows', 'mp')
All inputs are finite; a program needn't handle non-finite values.
Results may differ from a plain program's by a relative error of at most 0.0041.
Values may be sent and summed in bfloat16 or wider, within the bound.
A program may use at most 128 MiB of HBM per device.

v0:
```python
import jax
import jax.numpy as jnp
from jax import lax
from jax.sharding import PartitionSpec as P

D = 6144
floor_value = 0.1


def normalize(as_float, moment_sum, square_sum, gain, width):
    row_mean = moment_sum / width
    row_var = jnp.maximum(square_sum / width - row_mean * row_mean, 0.0)
    inverse = lax.rsqrt(row_var + floor_value)
    return ((as_float - row_mean[:, None]) * inverse[:, None] * gain[None, :]).astype(jnp.bfloat16)


def body(tokens, norm_gain, hidden_bias, weight_in, weight_out):
    as_float = tokens.astype(jnp.float32)
    moment_sum, square_sum = lax.psum(
        (jnp.sum(as_float, axis=1), jnp.sum(as_float * as_float, axis=1)), "mp"
    )
    local_gain = lax.dynamic_slice_in_dim(
        norm_gain, lax.axis_index("mp") * tokens.shape[1], tokens.shape[1]
    )
    shard_norm = normalize(as_float, moment_sum, square_sum, local_gain, D)
    normed = lax.all_gather(shard_norm, "mp", axis=1, tiled=True)
    shuffled = lax.all_to_all(normed, "rows", split_axis=1, concat_axis=0, tiled=True)
    preact = lax.psum_scatter(
        jnp.dot(shuffled, weight_in, preferred_element_type=jnp.float32),
        "rows",
        scatter_dimension=0,
        tiled=True,
    )
    hidden = jax.nn.gelu(preact + hidden_bias[None, :], approximate=False).astype(jnp.bfloat16)
    terms = jnp.dot(
        hidden,
        lax.all_gather(weight_out, "rows", axis=1, tiled=True),
        preferred_element_type=jnp.float32,
    )
    branch = lax.psum_scatter(terms, "mp", scatter_dimension=1, tiled=True)
    return (as_float + branch).astype(jnp.bfloat16)


def solution(mesh):
    return jax.shard_map(
        body,
        mesh=mesh,
        in_specs=(P("rows", "mp"), P(), P("mp"), P("rows", "mp"), P("mp", "rows")),
        out_specs=P("rows", "mp"),
        check_vma=False,
    )
```

profile of v0, /device:TPU:0, one launch (start us, length us, event | category | flops | bytes accessed | tf_op | source)
XLA Modules:
  0.0 561.1 jit_solution(460465434844182383)
XLA Ops:
  6.5 0.0 all-gather.3.cloned.1.call-start
  6.5 1.1 convert_reduce_fusion
  7.6 18.1 %all-reduce = (f32[128]{0:T(128)S(1)}, f32[128]{0:T(128)S(1)}) all-reduce(f32[128]{0:T(128)S(1)} %get-tuple-element.6, f32[128]{0:T(128)S(1)} %get-tuple-element.5), channel_id=1, replica_groups=mesh['rows'=4,'mp'=8] {'mp'}, use_global_device_ids=true, to_apply=%region_3.0 | all-reduce | flops 256 | bytes 2048 | tf_op jit(solution)/shard_map/psum | solution.py:19
  25.7 0.8 dynamic_slice.3
  26.5 1.8 fusion.45
  28.3 0.0 all-gather.3.cloned.1.call-update
  28.3 0.0 reduce-scatter.3.cloned.1.call-start
  28.3 23.6 %all-gather.3.cloned.1.call-done = bf16[128,6144]{1,0:T(8,128)(2,1)} async-done(((bf16[128,768]{1,0:T(8,128)(2,1)}), bf16[128,6144]{1,0:T(8,128)(2,1)}) %all-gather.3.cloned.1.call-update) | async-done | bytes 1572880 | tf_op jit(solution)/shard_map/all_gather | solution.py:26
  51.9 1.5 copy.9
  53.4 23.6 %all_to_all.19 = bf16[128,4,1536]{2,0,1:T(8,128)(2,1)S(1)} all-to-all(bf16[128,4,1536]{2,0,1:T(8,128)(2,1)S(1)} %bitcast.10), channel_id=1, replica_groups=mesh['rows'=4,'mp'=8] {'rows'}, dimensions={1} | all-to-all | bytes 3145728 | tf_op jit(solution)/shard_map/all_to_all | solution.py:27
  77.0 10.6 %fusion.78 = f32[512,3072]{1,0:T(8,128)} fusion(bf16[512,1536]{1,0:T(8,128)(2,1)S(1)} %bitcast.12, bf16[1536,3072]{1,0:T(8,128)(2,1)} %param.8), kind=kOutput, calls=%fused_computation.93 | convolution fusion | flops 4831838208 | bytes 17301504 | tf_op jit(solution)/shard_map/dot_general | solution.py:29
  87.6 0.0 reduce-scatter.3.cloned.1.call-update
  87.6 0.0 copy-start.1
  87.6 0.0 all-gather.5.cloned.1.call-start
  87.7 0.7 all-gather.5.cloned.1.call-update
  88.4 0.0 reduce-scatter.5.cloned.1.call-start
  88.4 67.0 %reduce-scatter.3.cloned.1.call-done = f32[128,3072]{1,0:T(8,128)} async-done(((f32[512,3072]{1,0:T(8,128)}), f32[128,3072]{1,0:T(8,128)}) %reduce-scatter.3.cloned.1.call-update) | async-done | bytes 1572880 | tf_op jit(solution)/shard_map/reduce_scatter | solution.py:28
  155.5 334.7 %all-gather.5.cloned.1.call-done = bf16[3072,6144]{1,0:T(8,128)(2,1)} async-done(((bf16[3072,1536]{1,0:T(8,128)(2,1)}), bf16[3072,6144]{1,0:T(8,128)(2,1)}) %all-gather.5.cloned.1.call-update) | async-done | bytes 37748752 | tf_op jit(solution)/shard_map/all_gather | solution.py:37
  490.2 0.0 copy-done.1
  490.2 22.1 %fusion.10 = f32[128,6144]{1,0:T(8,128)} fusion(bf16[3072,6144]{1,0:T(8,128)(2,1)} %all-gather.5.cloned.1.call-done, f32[128,3072]{1,0:T(8,128)} %reduce-scatter.3.cloned.1.call-done, f32[3072]{0:T(1024)S(1)} %copy-done.1), kind=kOutput, calls=%fused_computation.20 | convolution fusion | flops 4857790464 | bytes 42479616 | tf_op jit(solution)/shard_map/dot_general | solution.py:35
  512.3 0.0 copy-start
  512.3 0.0 reduce-scatter.5.cloned.1.call-update
  512.3 40.5 %reduce-scatter.5.cloned.1.call-done = f32[128,768]{1,0:T(8,128)} async-done(((f32[128,6144]{1,0:T(8,128)}), f32[128,768]{1,0:T(8,128)}) %reduce-scatter.5.cloned.1.call-update) | async-done | bytes 393232 | tf_op jit(solution)/shard_map/reduce_scatter | solution.py:40
  552.8 0.0 copy-done
  552.8 1.7 fusion.47
  (1 shorter events, 0.0 us)
Async XLA Ops:
  6.5 45.4 %all-gather.3.cloned.1.call-start = ((), (), s32[]{:S(2)}) async-start(), calls=%async_computation.3 | async-start | bytes 1769472 | tf_op jit(solution)/shard_map/all_gather | solution.py:26
  28.3 127.2 %reduce-scatter.3.cloned.1.call-start = ((), (), s32[]{:S(2)}) async-start(), calls=%async_computation.4 | async-start | bytes 7864320 | tf_op jit(solution)/shard_map/reduce_scatter | solution.py:28
  87.6 402.6 %copy-start.1 = (f32[3072]{0:T(1024)S(1)}, f32[3072]{0:T(1024)}, u32[]{:S(2)}) copy-start(f32[3072]{0:T(1024)} %param.7) | copy-start | bytes 36868
  87.6 402.6 %all-gather.5.cloned.1.call-start = ((), (), s32[]{:S(2)}) async-start(), calls=%async_computation.5 | async-start | bytes 47185920 | tf_op jit(solution)/shard_map/all_gather | solution.py:37
  88.4 464.4 %reduce-scatter.5.cloned.1.call-start = ((), (), s32[]{:S(2)}) async-start(), calls=%async_computation.6 | async-start | bytes 3538944 | tf_op jit(solution)/shard_map/reduce_scatter | solution.py:40
  512.3 40.6 %copy-start = (bf16[128,768]{1,0:T(8,128)(2,1)S(1)}, bf16[128,768]{1,0:T(8,128)(2,1)}, u32[]{:S(2)}) copy-start(bf16[128,768]{1,0:T(8,128)(2,1)} %param.5) | copy-start | bytes 589828
Sparse Core Ops, SparseCore 0:
  28.4 23.4 all-gather.2
  87.7 67.6 reduce-scatter.2
  157.3 332.8 all-gather.4
  512.4 40.3 reduce-scatter.4
where the time goes:
time: 561 us
  waiting for transfers between devices  467 us (83%)
  blocking collectives  41.7 us (7%)
  matrix products  32.6 us (6%)
  between operations  13.2 us (2%)
    all_gather x1, waiting for transfers between devices, body(): lax.all_gather(weight_out, 'rows', axis=1, tiled=True)  335 us
    reduce_scatter x1, waiting for transfers between devices, body(): lax.psum_scatter(jnp.dot(shuffled, weight_in, preferred_element_type=jnp....  67 us
    reduce_scatter x1, waiting for transfers between devices, body(): branch = lax.psum_scatter(terms, 'mp', scatter_dimension=1, tiled=True)  40.5 us
    all_to_all x1, blocking collectives, body(): lax.all_to_all(normed, 'rows', split_axis=1, concat_axis=0, tiled=True)  23.6 us
    all_gather x1, waiting for transfers between devices, body(): normed = lax.all_gather(shard_norm, 'mp', axis=1, tiled=True)  23.6 us
    dot_general x1, matrix products, body(): jnp.dot(hidden, lax.all_gather(weight_out, 'rows', axis=1, tiled=True), p...  22.1 us
    psum x1, blocking collectives, body(): lax.psum((jnp.sum(as_float, axis=1), jnp.sum(as_float * as_float, axis=1)...  18.1 us
  transfers between devices with their start and end apart: 4, of which 4 were waited for; matrix products, arithmetic and copies ran while one was open for 0% of the time, Pallas kernels for 0%

commit v1 on v0

--- a/solution.py
+++ b/solution.py
@@ -5,6 +5,18 @@
 
 D = 6144
 floor_value = 0.1
+
+
+def doubled_up(value, axis, dim):
+    ways, here = (lax.axis_size(axis), lax.axis_index(axis))
+    grown, reach = (value, 1)
+    while reach < ways:
+        theirs = lax.ppermute(grown, axis, [(d, d ^ reach) for d in range(ways)])
+        mine_first = jnp.concatenate([grown, theirs], axis=dim)
+        theirs_first = jnp.concatenate([theirs, grown], axis=dim)
+        grown = jnp.where(here & reach == 0, mine_first, theirs_first)
+        reach = 2 * reach
+    return grown
 
 
 def normalize(as_float, moment_sum, square_sum, gain, width):
@@ -32,11 +44,7 @@
         tiled=True,
     )
     hidden = jax.nn.gelu(preact + hidden_bias[None, :], approximate=False).astype(jnp.bfloat16)
-    terms = jnp.dot(
-        hidden,
-        lax.all_gather(weight_out, "rows", axis=1, tiled=True),
-        preferred_element_type=jnp.float32,
-    )
+    terms = jnp.dot(hidden, doubled_up(weight_out, "rows", 1), preferred_element_type=jnp.float32)
     branch = lax.psum_scatter(terms, "mp", scatter_dimension=1, tiled=True)
     return (as_float + branch).astype(jnp.bfloat16)
 

time: 561 us -> 825 us (1.47)
  blocking collectives: 41.7 us -> 396 us
  waiting for transfers between devices: 467 us -> 338 us
  other arithmetic: 4.54 us -> 23 us
  matrix products: 32.6 us -> 48.2 us
    all_to_all x1, blocking collectives: 23.6 us -> 380 us  [body(): lax.all_to_all(normed, 'rows', split_axis=1, concat_axis=0, tiled=True)]
    all_gather x1 -> x0, waiting for transfers between devices: 335 us -> none  [body(): lax.all_gather(weight_out, 'rows', axis=1, tiled=True)]
    ppermute x0 -> x2, waiting for transfers between devices: none -> 203 us  [doubled_up(): theirs = lax.ppermute(grown, axis, [(d, d ^ reach) for d in range(ways)])]
    select_n x0 -> x1, other arithmetic: none -> 20.3 us  [doubled_up(): grown = jnp.where(here & reach == 0, mine_first, theirs_first)]
    dot_general x1, matrix products: 22.1 us -> 37.7 us  [body(): jnp.dot(hidden, doubled_up(weight_out, 'rows', 1), preferred_element_type...]
  transfers between devices with their start and end apart: 4 -> 5, of which waited for: 4 -> 4; matrix products, arithmetic and copies ran while one was open for 0% -> 2% of each run, Pallas kernels for 0% -> 0%
where the time goes in v1:
time: 825 us
  blocking collectives  396 us (48%)
  waiting for transfers between devices  338 us (41%)
  matrix products  48.2 us (6%)
  other arithmetic  23 us (3%)
  between operations  13.1 us (2%)
    all_to_all x1, blocking collectives, body(): lax.all_to_all(normed, 'rows', split_axis=1, concat_axis=0, tiled=True)  380 us
    ppermute x2, waiting for transfers between devices, doubled_up(): theirs = lax.ppermute(grown, axis, [(d, d ^ reach) for d in range(ways)])  203 us
    reduce_scatter x1, waiting for transfers between devices, body(): lax.psum_scatter(jnp.dot(shuffled, weight_in, preferred_element_type=jnp....  71.3 us
    reduce_scatter x1, waiting for transfers between devices, body(): branch = lax.psum_scatter(terms, 'mp', scatter_dimension=1, tiled=True)  40.5 us
    dot_general x1, matrix products, body(): jnp.dot(hidden, doubled_up(weight_out, 'rows', 1), preferred_element_type...  37.7 us
    all_gather x1, waiting for transfers between devices, body(): normed = lax.all_gather(shard_norm, 'mp', axis=1, tiled=True)  22.6 us
    select_n x1, other arithmetic, doubled_up(): grown = jnp.where(here & reach == 0, mine_first, theirs_first)  20.3 us
  transfers between devices with their start and end apart: 5, of which 4 were waited for; matrix products, arithmetic and copies ran while one was open for 2% of the time, Pallas kernels for 0%

profile of v1, /device:TPU:0, one launch (start us, length us, event | category | flops | bytes accessed | tf_op | source)
XLA Modules:
  0.0 824.9 jit_solution(16975063714818692615)
XLA Ops:
  6.5 0.0 all-gather.2.cloned.1.call-start
  6.5 3.0 collective-permute-start
  9.5 0.0 copy-start
  9.5 203.2 %collective-permute-done = bf16[3072,1536]{1,0:T(8,128)(2,1)} collective-permute-done((bf16[3072,1536]{1,0:T(8,128)(2,1)}, bf16[3072,1536]{1,0:T(8,128)(2,1)}, u32[]{:S(2)}, u32[]{:S(2)}) %collective-permute-start) | collective-permute-done | bytes 9437216 | tf_op jit(solution)/shard_map/ppermute | solution.py:14
  212.7 20.3 %maximum_select_fusion.2 = bf16[3072,3072]{1,0:T(8,128)(2,1)} fusion(bf16[3072,1536]{1,0:T(8,128)(2,1)} %collective-permute-done, bf16[3072,1536]{1,0:T(8,128)(2,1)} %param.9, pred[]{:T(512)S(6)} %eq.7), kind=kLoop, calls=%fused_computation.8 | loop fusion | flops 84934656 | bytes 37748736 | tf_op jit(solution)/shard_map/jit(_where)/select_n | solution.py:17
  233.1 1.8 collective-permute-start.1
  234.9 0.8 dynamic_slice.3
  235.7 0.0 copy-done
  235.7 0.1 convert_reduce_fusion
  235.8 15.5 %all-reduce = (f32[128]{0:T(128)S(1)}, f32[128]{0:T(128)S(1)}) all-reduce(f32[128]{0:T(128)S(1)} %get-tuple-element.6, f32[128]{0:T(128)S(1)} %get-tuple-element.5), channel_id=1, replica_groups=mesh['rows'=4,'mp'=8] {'mp'}, use_global_device_ids=true, to_apply=%region_3.0 | all-reduce | flops 256 | bytes 2048 | tf_op jit(solution)/shard_map/psum | solution.py:31
  251.3 0.8 fusion.51
  252.1 0.0 all-gather.2.cloned.1.call-update
  252.2 0.0 reduce-scatter.3.cloned.1.call-start
  252.2 22.6 %all-gather.2.cloned.1.call-done = bf16[128,6144]{1,0:T(8,128)(2,1)} async-done(((bf16[128,768]{1,0:T(8,128)(2,1)}), bf16[128,6144]{1,0:T(8,128)(2,1)}) %all-gather.2.cloned.1.call-update) | async-done | bytes 1572880 | tf_op jit(solution)/shard_map/all_gather | solution.py:38
  274.8 1.5 copy.9
  276.4 380.1 %all_to_all.19 = bf16[128,4,1536]{2,0,1:T(8,128)(2,1)S(1)} all-to-all(bf16[128,4,1536]{2,0,1:T(8,128)(2,1)S(1)} %bitcast.9), channel_id=1, replica_groups=mesh['rows'=4,'mp'=8] {'rows'}, dimensions={1} | all-to-all | bytes 3145728 | tf_op jit(solution)/shard_map/all_to_all | solution.py:39
  656.5 10.6 %fusion.85 = f32[512,3072]{1,0:T(8,128)} fusion(bf16[512,1536]{1,0:T(8,128)(2,1)S(1)} %bitcast.11, bf16[1536,3072]{1,0:T(8,128)(2,1)} %param.8), kind=kOutput, calls=%fused_computation.102 | convolution fusion | flops 4831838208 | bytes 17301504 | tf_op jit(solution)/shard_map/dot_general | solution.py:41
  667.1 0.0 copy-start.1
  667.1 0.0 reduce-scatter.3.cloned.1.call-update
  667.1 0.0 reduce-scatter.5.cloned.1.call-start
  667.2 71.3 %reduce-scatter.3.cloned.1.call-done = f32[128,3072]{1,0:T(8,128)} async-done(((f32[512,3072]{1,0:T(8,128)}), f32[128,3072]{1,0:T(8,128)}) %reduce-scatter.3.cloned.1.call-update) | async-done | bytes 1572880 | tf_op jit(solution)/shard_map/reduce_scatter | solution.py:40
  738.5 0.0 collective-permute-done.1
  738.5 0.0 copy-done.1
  738.5 37.7 %fusion = f32[128,6144]{1,0:T(8,128)} fusion(bf16[3072,3072]{1,0:T(8,128)(2,1)} %collective-permute-done.1, bf16[3072,3072]{1,0:T(8,128)(2,1)} %maximum_select_fusion.2, pred[]{:T(512)S(6)} %eq.6, f32[128,3072]{1,0:T(8,128)} %reduce-scatter.3.cloned.1.call-done, f32[3072]{0:T(1024)S(1)} %copy-done.1), kind=kOutput, calls=%fused_computation.1 | convolution fusion | flops 5027659776 | bytes 42479616 | tf_op jit(solution)/shard_map/dot_general | solution.py:47
  776.2 0.0 reduce-scatter.5.cloned.1.call-update
  776.2 40.5 %reduce-scatter.5.cloned.1.call-done = f32[128,768]{1,0:T(8,128)} async-done(((f32[128,6144]{1,0:T(8,128)}), f32[128,768]{1,0:T(8,128)}) %reduce-scatter.5.cloned.1.call-update) | async-done | bytes 393232 | tf_op jit(solution)/shard_map/reduce_scatter | solution.py:48
  816.7 1.7 fusion.53
  (1 shorter events, 0.0 us)
Async XLA Ops:
  6.5 268.3 %all-gather.2.cloned.1.call-start = ((), (), s32[]{:S(2)}) async-start(), calls=%async_computation.3 | async-start | bytes 1769472 | tf_op jit(solution)/shard_map/all_gather | solution.py:38
  6.5 206.2 %collective-permute-start = (bf16[3072,1536]{1,0:T(8,128)(2,1)}, bf16[3072,1536]{1,0:T(8,128)(2,1)}, u32[]{:S(2)}, u32[]{:S(2)}) collective-permute-start(bf16[3072,1536]{1,0:T(8,128)(2,1)} %param.9), channel_id=1, source_target_pairs={{0,8},{8,0},{16,24},{24,16},{1,9},{9,1},{17,25},{25,17},{2,10},{10... | collective-permute-start | bytes 28311560 | tf_op jit(solution)/shard_map/ppermute | solution.py:14
  9.5 226.2 %copy-start = (bf16[128,768]{1,0:T(8,128)(2,1)S(1)}, bf16[128,768]{1,0:T(8,128)(2,1)}, u32[]{:S(2)}) copy-start(bf16[128,768]{1,0:T(8,128)(2,1)} %param.5) | copy-start | bytes 589828
  233.1 505.4 %collective-permute-start.1 = (bf16[3072,3072]{1,0:T(8,128)(2,1)}, bf16[3072,3072]{1,0:T(8,128)(2,1)}, u32[]{:S(2)}, u32[]{:S(2)}) collective-permute-start(bf16[3072,3072]{1,0:T(8,128)(2,1)} %maximum_select_fusion.2), channel_id=1, source_target_pairs={{0,16},{8,24},{16,0},{24,8},{1,17},{9,25},{17,1},{25,9},{2,18},{10... | collective-permute-start | bytes 56623112 | tf_op jit(solution)/shard_map/ppermute | solution.py:14
  252.2 486.3 %reduce-scatter.3.cloned.1.call-start = ((), (), s32[]{:S(2)}) async-start(), calls=%async_computation.4 | async-start | bytes 7864320 | tf_op jit(solution)/shard_map/reduce_scatter | solution.py:40
  667.1 71.4 %copy-start.1 = (f32[3072]{0:T(1024)S(1)}, f32[3072]{0:T(1024)}, u32[]{:S(2)}) copy-start(f32[3072]{0:T(1024)} %param.7) | copy-start | bytes 36868
  667.1 149.6 %reduce-scatter.5.cloned.1.call-start = ((), (), s32[]{:S(2)}) async-start(), calls=%async_computation.5 | async-start | bytes 3538944 | tf_op jit(solution)/shard_map/reduce_scatter | solution.py:48
Sparse Core Ops, SparseCore 0:
  252.3 22.5 all-gather.1
  667.2 71.2 reduce-scatter.2
  776.3 40.3 reduce-scatter.4
